TPU v7x, 32 devices: a whole 2x2x4 slice. The times are simulated.
32 devices in a mesh: grp: 2 (over y), blk: 4 (over z), uly: 4 (over x, core).
Axes of the slice: x: 2, y: 2, z: 4, core: 2. Of those that a mesh axis runs over, the one named last changes fastest.
Arguments:
- qkv: bfloat16 [2, 8, 16, 3, 32, 128], P('grp', 'blk', 'uly'), parts along dimension 0, may hold values from -6 to 6
- out_weight: bfloat16 [4096, 256], replicated, may hold values from -0.25 to 0.25
- lift_weight: bfloat16 [64, 512], P(None, 'uly'), may hold values from -0.75 to 0.75
- conv_weight: bfloat16 [4, 3, 3, 512, 512], P(None, None, None, 'uly'), may hold values from -0.15625 to 0.15625
Outputs:
- pixels: bfloat16 [2, 16, 32, 512], P('grp', 'blk', None, 'uly'), parts along dimension 0
There are 2 independent parts, one for each index of `grp`. A program takes and returns all parts, laid end to end along the dimension named above; an argument that names none is the same for every part. Nothing has to cross between parts.
All inputs are finite; a program needn't handle non-finite values.
Results may differ from a plain program's by a relative error of at most 0.02.
Values may be sent and summed in bfloat16 or wider, within the bound.
No kernel may reach another device: no remote copies, remote signals or barrier semaphores. Data moves between devices by JAX's collectives and lax.ppermute only.
A program may use at most 64 MiB of HBM per device.

v0:
```python
import functools

import jax
import jax.numpy as jnp
from jax import lax
from jax.sharding import PartitionSpec as P

PATCH = 2
LAYERS = 4


def with_halo(cells, sides, width):
    for axis, dim in sides:
        count = lax.axis_size(axis)
        ends = count - 1
        head = lax.slice_in_dim(cells, 0, width, axis=dim)
        tail = lax.slice_in_dim(cells, cells.shape[dim] - width, cells.shape[dim], axis=dim)
        cells = jnp.concatenate(
            [
                lax.ppermute(tail, axis, [(i, (i + 1) % count) for i in range(ends)]),
                cells,
                lax.ppermute(head, axis, [((i + 1) % count, i) for i in range(ends)]),
            ],
            axis=dim,
        )
    return cells


def online_update(carry, pieces, start, queries, scale):
    highest, totals, summed = carry
    keys = pieces[0].reshape(-1, pieces[0].shape[-2], pieces[0].shape[-1])
    values = pieces[1].reshape(-1, pieces[1].shape[-2], pieces[1].shape[-1])
    scores = jnp.einsum("qhd,khd->hqk", queries, keys, preferred_element_type=jnp.float32) * scale
    new_high = jnp.maximum(highest, jnp.max(scores, axis=2))
    weights = jnp.exp(scores - new_high[:, :, None])
    totals = jnp.sum(weights, axis=2)
    update = jnp.einsum(
        "hqk,khd->qhd", weights.astype(jnp.bfloat16), values, preferred_element_type=jnp.float32
    )
    summed = update
    return (new_high, totals, summed)


def attention_start(flat_queries):
    count, heads, size = flat_queries.shape
    return (
        jnp.full((heads, count), -1e30, jnp.float32),
        jnp.zeros((heads, count), jnp.float32),
        jnp.zeros((count, heads, size), jnp.float32),
    )


def attention_finish(carry, shape):
    highest, totals, summed = carry
    return (summed / jnp.transpose(totals)[:, :, None]).astype(jnp.bfloat16).reshape(shape)


def unfold_patches(piece, latent_ch):
    frames, rows, cols = (piece.shape[0], piece.shape[1], piece.shape[2])
    spread = piece.reshape(frames, rows, cols, PATCH, PATCH, latent_ch)
    spread = jnp.transpose(spread, (0, 1, 3, 2, 4, 5))
    return spread.reshape(frames, rows * PATCH, cols * PATCH, latent_ch)


def conv_layer(current, kernels):
    rims = with_halo(current, (("blk", 1),), 1)
    frames, height, width, outputs = current.shape
    empty = jnp.zeros((frames, height, width, outputs), jnp.float32)
    summed = empty
    padded = jnp.pad(
        lax.all_gather(rims, "uly", axis=3, tiled=True), ((0, 0), (0, 0), (1, 1), (0, 0))
    )
    for above in range(3):
        for beside in range(3):
            window = padded[:, above : above + height, beside : beside + width, :]
            summed = summed + jnp.einsum(
                "fyxc,dc->fyxd", window, kernels[above, beside], preferred_element_type=jnp.float32
            )
    return jax.nn.silu(summed).astype(jnp.bfloat16)


def body(qkv, out_weight, lift_weight, conv_weight):
    scale = 1.0 / qkv.shape[-1] ** 0.5
    grouped = lax.all_to_all(qkv, "blk", split_axis=4, concat_axis=1, tiled=True)
    queries = grouped[:, :, :, 0]
    flat_queries = queries.reshape(-1, queries.shape[3], queries.shape[4])
    folding = functools.partial(online_update, queries=flat_queries, scale=scale)
    carry = folding(
        attention_start(flat_queries),
        (
            lax.all_gather(grouped[:, :, :, 1], "uly", axis=2, tiled=True),
            lax.all_gather(grouped[:, :, :, 2], "uly", axis=2, tiled=True),
        ),
        jnp.int32(0),
    )
    attended = attention_finish(carry, queries.shape)
    restored = lax.all_to_all(attended, "blk", split_axis=1, concat_axis=3, tiled=True)
    frames, rows, cols = (restored.shape[0], restored.shape[1], restored.shape[2])
    features = restored.reshape(frames, rows, cols, restored.shape[3] * restored.shape[4])
    patches = jnp.einsum(
        "frcw,wp->frcp", features, out_weight, preferred_element_type=jnp.float32
    ).astype(jnp.bfloat16)
    latent_ch = lift_weight.shape[0]
    latent = unfold_patches(lax.all_gather(patches, "uly", axis=2, tiled=True), latent_ch)
    current = jnp.einsum(
        "fyxe,ed->fyxd", latent, lift_weight, preferred_element_type=jnp.float32
    ).astype(jnp.bfloat16)
    for layer in range(LAYERS):
        current = conv_layer(current, conv_weight[layer])
    return current


def solution(mesh):
    in_specs = (
        P("grp", "blk", "uly", None, None, None),
        P(),
        P(None, "uly"),
        P(None, None, None, "uly", None),
    )
    out_specs = P("grp", "blk", None, "uly")
    return jax.shard_map(body, mesh=mesh, in_specs=in_specs, out_specs=out_specs, check_vma=False)
```

profile of v0, /device:TPU:0, one launch (start us, length us, event | category | flops | bytes accessed | tf_op | source)
XLA Modules:
  0.0 105.2 jit_solution(9364590570968090370)
XLA Ops:
  0.0 1.2 %copy.17 = bf16[1,2,4,3,32,128]{5,2,3,1,0,4:T(4,128)(2,1)S(1)} copy(bf16[1,2,4,3,32,128]{5,4,3,2,1,0:T(8,128)(2,1)} %param.4) | data formatting | bytes 393216 | tf_op args[0]
  1.2 13.6 %all_to_all.33 = bf16[1,2,4,3,32,128]{5,2,3,1,0,4:T(4,128)(2,1)S(1)} all-to-all(bf16[1,2,4,3,32,128]{5,2,3,1,0,4:T(4,128)(2,1)S(1)} %copy.17), channel_id=1, replica_groups=mesh['grp'=2,'blk'=4,'uly'=4] {'blk'}, dimensions={4} | all-to-all | bytes 393216 | tf_op jit(solution)/shard_map/all_to_all | solution.py:84
  14.9 5.8 %all-gather = bf16[1,8,16,1,8,128]{5,4,3,1,0,2:T(8,128)(2,1)S(1)} all-gather(bf16[1,8,4,1,8,128]{5,4,3,1,0,2:T(8,128)(2,1)S(1)} %get-tuple-element.9), channel_id=2, replica_groups=mesh['grp'=2,'blk'=4,'uly'=4] {'uly'}, dimensions={2}, use_global_device_ids=true | all-gather | bytes 327680 | tf_op jit(solution)/shard_map/all_gather | solution.py:91
  20.9 0.3 fusion.114
  21.2 5.9 %all-gather.1 = bf16[1,8,16,1,8,128]{5,4,3,1,0,2:T(8,128)(2,1)S(1)} all-gather(bf16[1,8,4,1,8,128]{5,4,3,1,0,2:T(8,128)(2,1)S(1)} %get-tuple-element.10), channel_id=3, replica_groups=mesh['grp'=2,'blk'=4,'uly'=4] {'uly'}, dimensions={2}, use_global_device_ids=true | all-gather | bytes 327680 | tf_op jit(solution)/shard_map/all_gather | solution.py:92
  27.3 0.2 fusion.60
  27.5 0.2 fusion.3
  27.8 8.3 %all_to_all.34 = bf16[1,8,4,8,128]{4,2,3,0,1:T(4,128)(2,1)S(1)} all-to-all(bf16[1,8,4,8,128]{4,2,3,0,1:T(4,128)(2,1)S(1)} %copy.22), channel_id=1, replica_groups=mesh['grp'=2,'blk'=4,'uly'=4] {'blk'}, dimensions={1} | all-to-all | bytes 131072 | tf_op jit(solution)/shard_map/all_to_all | solution.py:97
  36.1 0.4 fusion.5
  36.5 5.2 %all-gather.2 = bf16[2,16,256]{2,0,1:T(2,128)(2,1)S(1)} all-gather(bf16[2,4,256]{2,0,1:T(2,128)(2,1)S(1)} %copy.24), channel_id=4, replica_groups=mesh['grp'=2,'blk'=4,'uly'=4] {'uly'}, dimensions={1}, use_global_device_ids=true | all-gather | bytes 20480 | tf_op jit(solution)/shard_map/all_gather | solution.py:104
  42.0 2.8 %collective-permute-start = (bf16[1,1,32,128]{3,2,1,0:T(8,128)(2,1)S(1)}, bf16[1,1,32,128]{3,2,1,0:T(8,128)(2,1)S(1)}, u32[]{:S(2)}, u32[]{:S(2)}) collective-permute-start(bf16[1,1,32,128]{3,2,1,0:T(8,128)(2,1)S(1)} %get-tuple-element.18), channel_id=1, source_target_pairs={{0,4},{4,8},{8,12},{1,5},{5,9},{9,13},{2,6},{6,10},{10,14},{3,7},{... | collective-permute-start | bytes 24584 | tf_op jit(solution)/shard_map/ppermute | solution.py:20
  44.8 1.3 %collective-permute-start.1 = (bf16[1,1,32,128]{3,2,1,0:T(8,128)(2,1)S(1)}, bf16[1,1,32,128]{3,2,1,0:T(8,128)(2,1)S(1)}, u32[]{:S(2)}, u32[]{:S(2)}) collective-permute-start(bf16[1,1,32,128]{3,2,1,0:T(8,128)(2,1)S(1)} %get-tuple-element.19), channel_id=1, source_target_pairs={{4,0},{8,4},{12,8},{5,1},{9,5},{13,9},{6,2},{10,6},{14,10},{7,3},{... | collective-permute-start | bytes 24584 | tf_op jit(solution)/shard_map/ppermute | solution.py:22
  46.1 2.6 %slice_bitcast_fusion = (bf16[3,3,128,512]{3,2,1,0:T(8,128)(2,1)S(1)}, bf16[3,3,128,512]{3,2,1,0:T(8,128)(2,1)S(1)}, bf16[3,3,128,512]{3,2,1,0:T(8,128)(2,1)S(1)}, bf16[3,3,128,512]{3,2,1,0:T(8,128)(2,1)S(1)}) fusion(bf16[4,3,3,128,512]{4,3,2,1,0:T(8,128)(2,1)} %param.7), kind=kLoop, calls=%fused_computation.2 | loop fusion | bytes 9437184 | tf_op jit(solution)/shard_map/squeeze | solution.py:109
  48.8 1.6 %collective-permute-done.1 = bf16[1,1,32,128]{3,2,1,0:T(8,128)(2,1)S(1)} collective-permute-done((bf16[1,1,32,128]{3,2,1,0:T(8,128)(2,1)S(1)}, bf16[1,1,32,128]{3,2,1,0:T(8,128)(2,1)S(1)}, u32[]{:S(2)}, u32[]{:S(2)}) %collective-permute-start.1) | collective-permute-done | bytes 8224 | tf_op jit(solution)/shard_map/ppermute | solution.py:22
  50.4 5.6 %all_gather.24 = bf16[1,6,32,512]{3,2,1,0:T(8,128)(2,1)S(1)} all-gather(bf16[1,6,32,128]{3,2,1,0:T(8,128)(2,1)S(1)} %pad_maximum_fusion), channel_id=1, replica_groups=mesh['grp'=2,'blk'=4,'uly'=4] {'uly'}, dimensions={3}, use_global_device_ids=true | all-gather | bytes 245760 | tf_op jit(solution)/shard_map/all_gather | solution.py:71
  57.5 0.2 fusion.80
  57.8 3.0 %collective-permute-start.2 = (bf16[1,1,32,128]{3,2,1,0:T(8,128)(2,1)S(1)}, bf16[1,1,32,128]{3,2,1,0:T(8,128)(2,1)S(1)}, u32[]{:S(2)}, u32[]{:S(2)}) collective-permute-start(bf16[1,1,32,128]{3,2,1,0:T(8,128)(2,1)S(1)} %get-tuple-element.16), channel_id=1, source_target_pairs={{0,4},{4,8},{8,12},{1,5},{5,9},{9,13},{2,6},{6,10},{10,14},{3,7},{... | collective-permute-start | bytes 24584 | tf_op jit(solution)/shard_map/ppermute | solution.py:20
  60.7 1.3 %collective-permute-start.3 = (bf16[1,1,32,128]{3,2,1,0:T(8,128)(2,1)S(1)}, bf16[1,1,32,128]{3,2,1,0:T(8,128)(2,1)S(1)}, u32[]{:S(2)}, u32[]{:S(2)}) collective-permute-start(bf16[1,1,32,128]{3,2,1,0:T(8,128)(2,1)S(1)} %get-tuple-element.17), channel_id=1, source_target_pairs={{4,0},{8,4},{12,8},{5,1},{9,5},{13,9},{6,2},{10,6},{14,10},{7,3},{... | collective-permute-start | bytes 24584 | tf_op jit(solution)/shard_map/ppermute | solution.py:22
  62.1 4.2 %collective-permute-done.3 = bf16[1,1,32,128]{3,2,1,0:T(8,128)(2,1)S(1)} collective-permute-done((bf16[1,1,32,128]{3,2,1,0:T(8,128)(2,1)S(1)}, bf16[1,1,32,128]{3,2,1,0:T(8,128)(2,1)S(1)}, u32[]{:S(2)}, u32[]{:S(2)}) %collective-permute-start.3) | collective-permute-done | bytes 8224 | tf_op jit(solution)/shard_map/ppermute | solution.py:22
  66.3 5.6 %all_gather.25 = bf16[1,6,32,512]{3,2,1,0:T(8,128)(2,1)S(1)} all-gather(bf16[1,6,32,128]{3,2,1,0:T(8,128)(2,1)S(1)} %pad_maximum_fusion.1), channel_id=1, replica_groups=mesh['grp'=2,'blk'=4,'uly'=4] {'uly'}, dimensions={3}, use_global_device_ids=true | all-gather | bytes 245760 | tf_op jit(solution)/shard_map/all_gather | solution.py:71
  72.9 0.2 convolution_add_fusion.19
  73.5 0.2 fusion.75
  73.7 2.3 %collective-permute-start.4 = (bf16[1,1,32,128]{3,2,1,0:T(8,128)(2,1)S(1)}, bf16[1,1,32,128]{3,2,1,0:T(8,128)(2,1)S(1)}, u32[]{:S(2)}, u32[]{:S(2)}) collective-permute-start(bf16[1,1,32,128]{3,2,1,0:T(8,128)(2,1)S(1)} %get-tuple-element.14), channel_id=1, source_target_pairs={{0,4},{4,8},{8,12},{1,5},{5,9},{9,13},{2,6},{6,10},{10,14},{3,7},{... | collective-permute-start | bytes 24584 | tf_op jit(solution)/shard_map/ppermute | solution.py:20
  76.0 1.3 %collective-permute-start.5 = (bf16[1,1,32,128]{3,2,1,0:T(8,128)(2,1)S(1)}, bf16[1,1,32,128]{3,2,1,0:T(8,128)(2,1)S(1)}, u32[]{:S(2)}, u32[]{:S(2)}) collective-permute-start(bf16[1,1,32,128]{3,2,1,0:T(8,128)(2,1)S(1)} %get-tuple-element.15), channel_id=1, source_target_pairs={{4,0},{8,4},{12,8},{5,1},{9,5},{13,9},{6,2},{10,6},{14,10},{7,3},{... | collective-permute-start | bytes 24584 | tf_op jit(solution)/shard_map/ppermute | solution.py:22
  77.4 4.2 %collective-permute-done.5 = bf16[1,1,32,128]{3,2,1,0:T(8,128)(2,1)S(1)} collective-permute-done((bf16[1,1,32,128]{3,2,1,0:T(8,128)(2,1)S(1)}, bf16[1,1,32,128]{3,2,1,0:T(8,128)(2,1)S(1)}, u32[]{:S(2)}, u32[]{:S(2)}) %collective-permute-start.5) | collective-permute-done | bytes 8224 | tf_op jit(solution)/shard_map/ppermute | solution.py:22
  81.6 5.6 %all_gather.26 = bf16[1,6,32,512]{3,2,1,0:T(8,128)(2,1)S(1)} all-gather(bf16[1,6,32,128]{3,2,1,0:T(8,128)(2,1)S(1)} %pad_maximum_fusion.2), channel_id=1, replica_groups=mesh['grp'=2,'blk'=4,'uly'=4] {'uly'}, dimensions={3}, use_global_device_ids=true | all-gather | bytes 245760 | tf_op jit(solution)/shard_map/all_gather | solution.py:71
  88.7 0.2 fusion.70
  89.0 2.6 %collective-permute-start.6 = (bf16[1,1,32,128]{3,2,1,0:T(8,128)(2,1)S(1)}, bf16[1,1,32,128]{3,2,1,0:T(8,128)(2,1)S(1)}, u32[]{:S(2)}, u32[]{:S(2)}) collective-permute-start(bf16[1,1,32,128]{3,2,1,0:T(8,128)(2,1)S(1)} %get-tuple-element.12), channel_id=1, source_target_pairs={{0,4},{4,8},{8,12},{1,5},{5,9},{9,13},{2,6},{6,10},{10,14},{3,7},{... | collective-permute-start | bytes 24584 | tf_op jit(solution)/shard_map/ppermute | solution.py:20
  91.6 1.3 %collective-permute-start.7 = (bf16[1,1,32,128]{3,2,1,0:T(8,128)(2,1)S(1)}, bf16[1,1,32,128]{3,2,1,0:T(8,128)(2,1)S(1)}, u32[]{:S(2)}, u32[]{:S(2)}) collective-permute-start(bf16[1,1,32,128]{3,2,1,0:T(8,128)(2,1)S(1)} %get-tuple-element.13), channel_id=1, source_target_pairs={{4,0},{8,4},{12,8},{5,1},{9,5},{13,9},{6,2},{10,6},{14,10},{7,3},{... | collective-permute-start | bytes 24584 | tf_op jit(solution)/shard_map/ppermute | solution.py:22
  93.0 4.2 %collective-permute-done.7 = bf16[1,1,32,128]{3,2,1,0:T(8,128)(2,1)S(1)} collective-permute-done((bf16[1,1,32,128]{3,2,1,0:T(8,128)(2,1)S(1)}, bf16[1,1,32,128]{3,2,1,0:T(8,128)(2,1)S(1)}, u32[]{:S(2)}, u32[]{:S(2)}) %collective-permute-start.7) | collective-permute-done | bytes 8224 | tf_op jit(solution)/shard_map/ppermute | solution.py:22
  97.2 5.6 %all_gather.27 = bf16[1,6,32,512]{3,2,1,0:T(8,128)(2,1)S(1)} all-gather(bf16[1,6,32,128]{3,2,1,0:T(8,128)(2,1)S(1)} %pad_maximum_fusion.3), channel_id=1, replica_groups=mesh['grp'=2,'blk'=4,'uly'=4] {'uly'}, dimensions={3}, use_global_device_ids=true | all-gather | bytes 245760 | tf_op jit(solution)/shard_map/all_gather | solution.py:71
  104.3 0.8 fusion.65
  (60 shorter events, 6.7 us)
Async XLA Ops:
  0.0 36.1 %copy-start = (bf16[4096,256]{1,0:T(8,128)(2,1)S(1)}, bf16[4096,256]{1,0:T(8,128)(2,1)}, u32[]{:S(2)}) copy-start(bf16[4096,256]{1,0:T(8,128)(2,1)} %param.5) | copy-start | bytes 6291460
  36.1 5.8 %copy-start.1 = (bf16[64,128]{1,0:T(8,128)(2,1)S(1)}, bf16[64,128]{1,0:T(8,128)(2,1)}, u32[]{:S(2)}) copy-start(bf16[64,128]{1,0:T(8,128)(2,1)} %param.6) | copy-start | bytes 49156
  42.0 6.8 %collective-permute-start = (bf16[1,1,32,128]{3,2,1,0:T(8,128)(2,1)S(1)}, bf16[1,1,32,128]{3,2,1,0:T(8,128)(2,1)S(1)}, u32[]{:S(2)}, u32[]{:S(2)}) collective-permute-start(bf16[1,1,32,128]{3,2,1,0:T(8,128)(2,1)S(1)} %get-tuple-element.18), channel_id=1, source_target_pairs={{0,4},{4,8},{8,12},{1,5},{5,9},{9,13},{2,6},{6,10},{10,14},{3,7},{... | collective-permute-start | bytes 24584 | tf_op jit(solution)/shard_map/ppermute | solution.py:20
  44.8 5.5 %collective-permute-start.1 = (bf16[1,1,32,128]{3,2,1,0:T(8,128)(2,1)S(1)}, bf16[1,1,32,128]{3,2,1,0:T(8,128)(2,1)S(1)}, u32[]{:S(2)}, u32[]{:S(2)}) collective-permute-start(bf16[1,1,32,128]{3,2,1,0:T(8,128)(2,1)S(1)} %get-tuple-element.19), channel_id=1, source_target_pairs={{4,0},{8,4},{12,8},{5,1},{9,5},{13,9},{6,2},{10,6},{14,10},{7,3},{... | collective-permute-start | bytes 24584 | tf_op jit(solution)/shard_map/ppermute | solution.py:22
  57.8 4.3 %collective-permute-start.2 = (bf16[1,1,32,128]{3,2,1,0:T(8,128)(2,1)S(1)}, bf16[1,1,32,128]{3,2,1,0:T(8,128)(2,1)S(1)}, u32[]{:S(2)}, u32[]{:S(2)}) collective-permute-start(bf16[1,1,32,128]{3,2,1,0:T(8,128)(2,1)S(1)} %get-tuple-element.16), channel_id=1, source_target_pairs={{0,4},{4,8},{8,12},{1,5},{5,9},{9,13},{2,6},{6,10},{10,14},{3,7},{... | collective-permute-start | bytes 24584 | tf_op jit(solution)/shard_map/ppermute | solution.py:20
  60.7 5.5 %collective-permute-start.3 = (bf16[1,1,32,128]{3,2,1,0:T(8,128)(2,1)S(1)}, bf16[1,1,32,128]{3,2,1,0:T(8,128)(2,1)S(1)}, u32[]{:S(2)}, u32[]{:S(2)}) collective-permute-start(bf16[1,1,32,128]{3,2,1,0:T(8,128)(2,1)S(1)} %get-tuple-element.17), channel_id=1, source_target_pairs={{4,0},{8,4},{12,8},{5,1},{9,5},{13,9},{6,2},{10,6},{14,10},{7,3},{... | collective-permute-start | bytes 24584 | tf_op jit(solution)/shard_map/ppermute | solution.py:22
  73.7 3.7 %collective-permute-start.4 = (bf16[1,1,32,128]{3,2,1,0:T(8,128)(2,1)S(1)}, bf16[1,1,32,128]{3,2,1,0:T(8,128)(2,1)S(1)}, u32[]{:S(2)}, u32[]{:S(2)}) collective-permute-start(bf16[1,1,32,128]{3,2,1,0:T(8,128)(2,1)S(1)} %get-tuple-element.14), channel_id=1, source_target_pairs={{0,4},{4,8},{8,12},{1,5},{5,9},{9,13},{2,6},{6,10},{10,14},{3,7},{... | collective-permute-start | bytes 24584 | tf_op jit(solution)/shard_map/ppermute | solution.py:20
  76.0 5.5 %collective-permute-start.5 = (bf16[1,1,32,128]{3,2,1,0:T(8,128)(2,1)S(1)}, bf16[1,1,32,128]{3,2,1,0:T(8,128)(2,1)S(1)}, u32[]{:S(2)}, u32[]{:S(2)}) collective-permute-start(bf16[1,1,32,128]{3,2,1,0:T(8,128)(2,1)S(1)} %get-tuple-element.15), channel_id=1, source_target_pairs={{4,0},{8,4},{12,8},{5,1},{9,5},{13,9},{6,2},{10,6},{14,10},{7,3},{... | collective-permute-start | bytes 24584 | tf_op jit(solution)/shard_map/ppermute | solution.py:22
  89.0 4.0 %collective-permute-start.6 = (bf16[1,1,32,128]{3,2,1,0:T(8,128)(2,1)S(1)}, bf16[1,1,32,128]{3,2,1,0:T(8,128)(2,1)S(1)}, u32[]{:S(2)}, u32[]{:S(2)}) collective-permute-start(bf16[1,1,32,128]{3,2,1,0:T(8,128)(2,1)S(1)} %get-tuple-element.12), channel_id=1, source_target_pairs={{0,4},{4,8},{8,12},{1,5},{5,9},{9,13},{2,6},{6,10},{10,14},{3,7},{... | collective-permute-start | bytes 24584 | tf_op jit(solution)/shard_map/ppermute | solution.py:20
  91.6 5.5 %collective-permute-start.7 = (bf16[1,1,32,128]{3,2,1,0:T(8,128)(2,1)S(1)}, bf16[1,1,32,128]{3,2,1,0:T(8,128)(2,1)S(1)}, u32[]{:S(2)}, u32[]{:S(2)}) collective-permute-start(bf16[1,1,32,128]{3,2,1,0:T(8,128)(2,1)S(1)} %get-tuple-element.13), channel_id=1, source_target_pairs={{4,0},{8,4},{12,8},{5,1},{9,5},{13,9},{6,2},{10,6},{14,10},{7,3},{... | collective-permute-start | bytes 24584 | tf_op jit(solution)/shard_map/ppermute | solution.py:22
where the time goes:
time: 106 us; the launch traced here: 105 us
  blocking collectives  61.2 us (58%)
  starting transfers between devices  15.9 us (15%)
  waiting for transfers between devices  14.3 us (13%)
  matrix products  8.44 us (8%)
  local copies, waits for them, and re-layouts  4.51 us (4%)
    all_gather x4, blocking collectives, conv_layer(): lax.all_gather(rims, 'uly', axis=3, tiled=True)  22.5 us
    ppermute x4, waiting for transfers between devices, with_halo(): lax.ppermute(head, axis, [((i + 1) % count, i) for i in range(ends)])  14.2 us
    all_to_all x1, blocking collectives, body(): lax.all_to_all(qkv, 'blk', split_axis=4, concat_axis=1, tiled=True)  13.6 us
    ppermute x4, starting transfers between devices, with_halo(): lax.ppermute(tail, axis, [(i, (i + 1) % count) for i in range(ends)])  10.8 us
    all_to_all x1, blocking collectives, body(): lax.all_to_all(attended, 'blk', split_axis=1, concat_axis=3, tiled=True)  8.26 us
    dot_general x36, matrix products, conv_layer(): jnp.einsum('fyxc,dc->fyxd', window, kernels[above, beside], preferred_ele...  7.35 us
    all_gather x1, blocking collectives, body(): lax.all_gather(grouped[:, :, :, 2], 'uly', axis=2, tiled=True)  5.85 us
    all_gather x1, blocking collectives, body(): lax.all_gather(grouped[:, :, :, 1], 'uly', axis=2, tiled=True)  5.78 us
  transfers between devices with their start and end apart: 8, of which 4 were waited for; matrix products, arithmetic and copies ran while one was open for 3% of the time, Pallas kernels for 0%

commit v1 on v0

v1 whole, which is shorter than its diff:
```python
import jax
import jax.numpy as jnp
from jax import lax
from jax.sharding import PartitionSpec as P

PATCH = 2
LAYERS = 4


def swap(pieces, axis):
    count = len(pieces)
    return [pieces[0]] + [
        lax.ppermute(pieces[step], axis, [(i, i ^ step) for i in range(count)])
        for step in range(1, count)
    ]


def spread(piece, axis):
    return swap([piece] * lax.axis_size(axis), axis)


def cut(array, start, size, axis):
    return lax.dynamic_slice_in_dim(array, start, size, axis=axis)


def attend(queries, keys, values):
    scale = 1.0 / queries.shape[-1] ** 0.5
    scores = jnp.einsum("hqd,hkd->hqk", queries, keys, preferred_element_type=jnp.float32) * scale
    weights = jnp.exp(scores - jnp.max(scores, axis=2, keepdims=True))
    totals = jnp.sum(weights, axis=2)
    mixed = jnp.einsum(
        "hqk,hkd->hqd", weights.astype(jnp.bfloat16), values, preferred_element_type=jnp.float32
    )
    return (mixed / totals[:, :, None]).astype(jnp.bfloat16)


def ordered(blocks, me):
    stacked = jnp.stack(blocks)
    return jnp.concatenate(
        [cut(stacked, me ^ place, 1, 0) for place in range(len(blocks))], axis=0
    )


def window_by_swaps(qkv, out_weight, reach):
    frames, rows, cols, _, heads, size = qkv.shape
    lines, sides = lax.axis_size("blk"), lax.axis_size("uly")
    line, side = lax.axis_index("blk"), lax.axis_index("uly")
    group, share = heads // sides, heads // sides // lines
    got = swap([cut(qkv, (side ^ s) * group, group, 4) for s in range(sides)], "uly")
    grouped = jnp.stack(got, axis=3)
    grouped = jnp.transpose(grouped, (4, 5, 0, 1, 3, 2, 6))
    got = swap([cut(grouped, (line ^ t) * share, share, 1) for t in range(lines)], "blk")
    shared = ordered(got, line)
    shared = jnp.transpose(shared, (1, 2, 3, 0, 4, 5, 6, 7))
    flat = shared.reshape(3, share, -1, size)
    attended = attend(flat[0], flat[1], flat[2])
    attended = attended.reshape(share, frames, lines * rows, sides * cols, size)
    attended = jnp.transpose(attended, (1, 2, 3, 0, 4)).reshape(
        frames, lines * rows, sides * cols, share * size
    )
    padded = jnp.pad(attended, ((0, 0), (reach, reach), (0, 0), (0, 0)))
    got = swap([cut(padded, (line ^ t) * rows, rows + 2 * reach, 1) for t in range(lines)], "blk")
    partial = 0.0
    for t in range(lines):
        weight = cut(out_weight, ((side * lines) + (line ^ t)) * share * size, share * size, 0)
        partial = partial + jnp.einsum(
            "frcw,wp->frcp", got[t], weight, preferred_element_type=jnp.float32
        )
    partial = partial.astype(jnp.bfloat16)
    got = spread(partial, "uly")
    blocks = []
    for place in range(sides):
        total = 0.0
        for s in range(sides):
            at = (place ^ s) * cols
            total = total + got[s][:, :, at : at + cols].astype(jnp.float32)
        blocks.append(total.astype(jnp.bfloat16))
    patches = ordered(blocks, side)
    patches = jnp.transpose(patches, (1, 2, 0, 3, 4))
    return patches.reshape(frames, rows + 2 * reach, sides * cols, -1)


def window_by_gathers(qkv, out_weight, reach):
    frames, rows, cols, _, heads, size = qkv.shape
    grouped = lax.all_to_all(qkv, "blk", split_axis=4, concat_axis=1, tiled=True)
    flat = [
        lax.all_gather(grouped[:, :, :, which], "uly", axis=2, tiled=True) for which in (1, 2)
    ]
    flat = [grouped[:, :, :, 0]] + flat
    flat = [jnp.swapaxes(one.reshape(-1, one.shape[3], size), 0, 1) for one in flat]
    attended = jnp.swapaxes(attend(*flat), 0, 1)
    attended = attended.reshape(grouped.shape[:3] + grouped.shape[4:])
    restored = lax.all_to_all(attended, "blk", split_axis=1, concat_axis=3, tiled=True)
    patches = jnp.einsum(
        "frcw,wp->frcp",
        restored.reshape(frames, rows, cols, heads * size),
        out_weight,
        preferred_element_type=jnp.float32,
    ).astype(jnp.bfloat16)
    patches = lax.all_gather(patches, "uly", axis=2, tiled=True)
    patches = lax.all_gather(patches, "blk", axis=1, tiled=True)
    padded = jnp.pad(patches, ((0, 0), (reach, reach), (0, 0), (0, 0)))
    return cut(padded, lax.axis_index("blk") * rows, rows + 2 * reach, 1)


def unfold_patches(piece, latent_ch):
    frames, rows, cols = (piece.shape[0], piece.shape[1], piece.shape[2])
    parts = piece.reshape(frames, rows, cols, PATCH, PATCH, latent_ch)
    parts = jnp.transpose(parts, (0, 1, 3, 2, 4, 5))
    return parts.reshape(frames, rows * PATCH, cols * PATCH, latent_ch)


def convolve(current, kernels):
    return lax.conv_general_dilated(
        current,
        kernels,
        (1, 1),
        ((0, 0), (1, 1)),
        dimension_numbers=("NHWC", "HWOI", "NHWC"),
        preferred_element_type=jnp.float32,
    )


def activate(summed, first, height):
    rows = first + lax.broadcasted_iota(jnp.int32, summed.shape, 1)
    inside = (rows >= 0) & (rows < height)
    return jnp.where(inside, jax.nn.silu(summed), 0.0).astype(jnp.bfloat16)


def body(qkv, out_weight, lift_weight, conv_weight):
    rows, heads = qkv.shape[1], qkv.shape[4]
    lines, sides = lax.axis_size("blk"), lax.axis_size("uly")
    side = lax.axis_index("uly")
    latent_ch = lift_weight.shape[0]
    own = conv_weight.shape[3]
    reach = -(-LAYERS // PATCH)
    lifts = spread(lift_weight, "uly")
    folded = 0.0
    for s in range(sides):
        kernels = cut(conv_weight[0], (side ^ s) * own, own, 3)
        folded = folded + jnp.einsum(
            "abdc,ec->abde", kernels, lifts[s], preferred_element_type=jnp.float32
        )
    folded = ordered(spread(folded.astype(jnp.bfloat16), "uly"), side)
    folded = jnp.transpose(folded, (1, 2, 0, 3, 4)).reshape(3, 3, sides * own, latent_ch)
    powers = lines & (lines - 1) == 0 and sides & (sides - 1) == 0
    if powers and heads % (lines * sides) == 0:
        patches = window_by_swaps(qkv, out_weight, reach)
    else:
        patches = window_by_gathers(qkv, out_weight, reach)
    height = lines * rows * PATCH
    margin = LAYERS - 1
    start = lax.axis_index("blk") * rows * PATCH
    latent = unfold_patches(patches, latent_ch)
    spare = reach * PATCH - LAYERS
    latent = latent[:, spare : latent.shape[1] - spare]
    current = activate(convolve(latent, folded), start - margin, height)
    for layer in range(1, LAYERS):
        margin -= 1
        kernels = conv_weight[layer]
        if layer > 1:
            current = jnp.concatenate(spread(current, "uly"), axis=3)
            kernels = jnp.concatenate(
                [cut(kernels, (side ^ s) * own, own, 3) for s in range(sides)], axis=3
            )
        current = activate(convolve(current, kernels), start - margin, height)
    return current


def solution(mesh):
    in_specs = (
        P("grp", "blk", "uly", None, None, None),
        P(),
        P(None, "uly"),
        P(None, None, None, "uly", None),
    )
    out_specs = P("grp", "blk", None, "uly")
    return jax.shard_map(body, mesh=mesh, in_specs=in_specs, out_specs=out_specs, check_vma=False)
```

time: 106 us -> 62.4 us (0.59)
  blocking collectives: 61.2 us -> 0 us
  starting transfers between devices: 15.9 us -> 21.9 us
  local copies, waits for them, and re-layouts: 4.51 us -> 9.95 us
  waiting for transfers between devices: 14.3 us -> 17.7 us
  other arithmetic: 0.24 us -> 2.43 us
    all_gather x7 -> x0, blocking collectives: 39.4 us -> none  [the longest x4 22.5 us: conv_layer(): lax.all_gather(rims, 'uly', axis=3, tiled=True)]
    all_to_all x2 -> x0, blocking collectives: 21.9 us -> none  [the longest x1 13.6 us: body(): lax.all_to_all(qkv, 'blk', split_axis=4, concat_axis=1, tiled=True)]
    ppermute x8 -> x24, starting transfers between devices: 15.9 us -> 21.9 us  [swap(): lax.ppermute(pieces[step], axis, [(i, i ^ step) for i in range(count)])]
    conv_general_dilated x0 -> x4, matrix products: none -> 4.23 us  [convolve(): lax.conv_general_dilated(current, kernels, (1, 1), ((0, 0), (1, 1)), dime...]
    slice x6 -> x5, local copies, waits for them, and re-layouts: 0.11 us -> 3.98 us  [the longest x1 3.75 us: body(): kernels = cut(conv_weight[0], (side ^ s) * own, own, 3)]
    dynamic_slice x0 -> x5, local copies, waits for them, and re-layouts: none -> 3.44 us  [cut(): return lax.dynamic_slice_in_dim(array, start, size, axis=axis)]
    ppermute x8 -> x24, waiting for transfers between devices: 14.3 us -> 17.7 us  [swap(): lax.ppermute(pieces[step], axis, [(i, i ^ step) for i in range(count)])]
    dot_general x40 -> x10, matrix products: 8.44 us -> 5.1 us  [the longest x4 4.08 us: body(): jnp.einsum('abdc,ec->abde', kernels, lifts[s], preferred_element_type=jnp...]
  transfers between devices with their start and end apart: 8 -> 24, of which waited for: 4 -> 12; matrix products, arithmetic and copies ran while one was open for 3% -> 25% of each run, Pallas kernels for 0% -> 0%
where the time goes in v1:
time: 62.4 us; the launch traced here: 62 us
  starting transfers between devices  21.9 us (35%)
  waiting for transfers between devices  17.7 us (28%)
  local copies, waits for them, and re-layouts  9.95 us (16%)
  matrix products  9.33 us (15%)
  other arithmetic  2.43 us (4%)
  between operations  0.64 us (1%)
    ppermute x24, starting transfers between devices, swap(): lax.ppermute(pieces[step], axis, [(i, i ^ step) for i in range(count)])  21.9 us
    ppermute x24, waiting for transfers between devices, swap(): lax.ppermute(pieces[step], axis, [(i, i ^ step) for i in range(count)])  17.7 us
    conv_general_dilated x4, matrix products, convolve(): lax.conv_general_dilated(current, kernels, (1, 1), ((0, 0), (1, 1)), dime...  4.23 us
    dot_general x4, matrix products, body(): jnp.einsum('abdc,ec->abde', kernels, lifts[s], preferred_element_type=jnp...  4.08 us
    slice x1, local copies, waits for them, and re-layouts, body(): kernels = cut(conv_weight[0], (side ^ s) * own, own, 3)  3.75 us
    dynamic_slice x5, local copies, waits for them, and re-layouts, cut(): return lax.dynamic_slice_in_dim(array, start, size, axis=axis)  3.44 us
  transfers between devices with their start and end apart: 24, of which 12 were waited for; matrix products, arithmetic and copies ran while one was open for 25% of the time, Pallas kernels for 0%

profile of v1, /device:TPU:0, one launch (start us, length us, event | category | flops | bytes accessed | tf_op | source)
XLA Modules:
  0.0 62.0 jit_solution(4402982230240321170)
XLA Ops:
  0.5 2.6 %collective-permute-start.14 = (bf16[64,128]{1,0:T(8,128)(2,1)}, bf16[64,128]{1,0:T(8,128)(2,1)}, u32[]{:S(2)}, u32[]{:S(2)}) collective-permute-start(bf16[64,128]{1,0:T(8,128)(2,1)} %param.6), channel_id=1, source_target_pairs={{0,3},{1,2},{2,1},{3,0},{4,7},{5,6},{6,5},{7,4},{8,11},{9,10},{10,... | collective-permute-start | bytes 49160 | tf_op jit(solution)/shard_map/ppermute | solution.py:13
  3.1 0.9 %dynamic-slice_bitcast_fusion.12 = (bf16[1,2,4,1,3,8,128]{6,5,4,2,1,3,0:T(8,128)(2,1)S(1)}, bf16[1,2,4,3,8,128]{5,4,3,2,1,0:T(8,128)(2,1)S(1)}, bf16[1,2,4,3,8,1...) fusion(bf16[1,2,4,3,32,128]{5,4,3,2,1,0:T(8,128)(2,1)} %param.4, s32[]{:T(128)S(6)} %select_n.112, ...), kind=kLoop, calls=%fused_computation.135 | loop fusion | bytes 393232 | tf_op jit(solution)/shard_map/stack | solution.py:50
  4.2 2.0 %collective-permute-start.1 = (bf16[1,2,4,3,8,128]{5,4,3,2,1,0:T(8,128)(2,1)S(1)}, bf16[1,2,4,3,8,128]{5,4,3,2,1,0:T(8,128)(2,1)}, u32[]{:S(2)}, u32[]{:S(2)}) collective-permute-start(bf16[1,2,4,3,8,128]{5,4,3,2,1,0:T(8,128)(2,1)S(1)} %get-tuple-element.40), channel_id=1, source_target_pairs={{0,2},{1,3},{2,0},{3,1},{4,6},{5,7},{6,4},{7,5},{8,10},{9,11},{10,... | collective-permute-start | bytes 147464 | tf_op jit(solution)/shard_map/ppermute | solution.py:13
  6.2 3.8 %fusion.143 = (bf16[1,3,3,128,512]{4,3,2,1,0:T(8,128)(2,1)S(1)}, bf16[1,3,3,128,512]{4,3,2,1,0:T(8,128)(2,1)}, bf16[1,3,3,128,512]{4,3,2,1,0:T(8,128)(2,1)}) fusion(bf16[4,3,3,128,512]{4,3,2,1,0:T(8,128)(2,1)} %param.7), kind=kLoop, calls=%fused_computation.190 | loop fusion | bytes 7077888 | tf_op jit(solution)/shard_map/slice | solution.py:140
  10.4 1.0 %fusion.66 = f32[3,3,128,64]{2,3,1,0:T(8,128)} fusion(bf16[1,3,3,128,512]{4,3,2,1,0:T(8,128)(2,1)S(1)} %get-tuple-element.5, s32[]{:T(128)S(6)} %select_n.136, bf16[64,128]{1,0:T(8,128)(2,1)S(1)} %copy-done.9), kind=kOutput, calls=%fused_computation.73 | convolution fusion | flops 18874368 | bytes 606212 | tf_op jit(solution)/shard_map/abdc,ec->abde/dot_general | solution.py:141
  11.4 3.1 %dynamic-slice_bitcast_fusion.3 = (bf16[3,3,128,128]{3,2,1,0:T(8,128)(2,1)}, bf16[3,3,128,128]{3,2,1,0:T(8,128)(2,1)}, bf16[3,3,128,128]{3,2,1,0:T(8,128)(2,1)},...) fusion(bf16[1,3,3,128,512]{4,3,2,1,0:T(8,128)(2,1)} %get-tuple-, ...), kind=kLoop, calls=%fused_computation.78 | loop fusion | bytes 4718608 | tf_op jit(solution)/shard_map/dynamic_slice | solution.py:23
  14.8 1.2 %convolution_add_fusion.1 = f32[3,3,128,64]{2,3,1,0:T(8,128)S(1)} fusion(f32[3,3,128,64]{2,3,1,0:T(8,128)} %fusion.66, bf16[1,3,3,128,512]{4,3,2,1,0:T(8,128)(2,1)S(1)} %get-tuple-element.5, s32[]{:T(128)S(6)} %select_n.137, bf16[64,128]{1,0:T(8,128)(2,1)S(1)} %collective-permute-done.12), kind=kOutput, calls=%fused_computation.22 | convolution fusion | flops 18948096 | bytes 901124 | tf_op jit(solution)/shard_map/abdc,ec->abde/dot_general | solution.py:141
  16.0 1.0 %fusion.62 = f32[3,3,128,64]{2,3,1,0:T(8,128)S(1)} fusion(bf16[1,3,3,128,512]{4,3,2,1,0:T(8,128)(2,1)S(1)} %get-tuple-element.5, s32[]{:T(128)S(6)} %select_n.139, bf16[64,128]{1,0:T(8,128)(2,1)} %collective-permute-done.14), kind=kOutput, calls=%fused_computation.69 | convolution fusion | flops 18874368 | bytes 606212 | tf_op jit(solution)/shard_map/abdc,ec->abde/dot_general | solution.py:141
  16.9 1.5 %collective-permute-done.2 = bf16[1,2,4,3,8,128]{5,4,3,2,1,0:T(8,128)(2,1)S(1)} collective-permute-done((bf16[1,2,4,3,8,128]{5,4,3,2,1,0:T(8,128)(2,1)S(1)}, bf16[1,2,4,3,8,128]{5,4,3,2,1,0:T(8,128)(2,1)S(1)}, u32[]{:S(2)}, u32[]{:S(2)}) %collective-permute-start.2) | collective-permute-done | bytes 49184 | tf_op jit(solution)/shard_map/ppermute | solution.py:13
  18.4 0.8 %pad_maximum_fusion.1 = bf16[1,2,4,4,3,8,128]{6,5,4,2,1,3,0:T(8,128)(2,1)S(1)} fusion(bf16[1,2,4,1,3,8,128]{6,5,4,2,1,3,0:T(8,128)(2,1)S(1)} %bitcast.194, bf16[1,2,4,1,3,8,128]{6,5,4,2,1,3,0:T(8,128)(2,1)} %bitcast.2, bf16[1,2,4,1,3,8,128]{6,5,4,2,1,3,0:T(8,128)(2,1)S(1)} %bitcast.190, bf16[1,2,4,1,3,8,128]{6,5,4,2,1,3,0:T(8,128)(2,1)S(1)} %get-tuple-element.37), kind=kLoop, calls=%fused_computation.91 | loop fusion | flops 294912 | bytes 393216 | tf_op jit(solution)/shard_map/stack | solution.py:50
  19.5 3.7 %collective-permute-start.5 = (bf16[3,2,1,2,4,4,128]{6,1,0,5,3,4,2:T(2,128)(2,1)S(1)}, bf16[3,2,1,2,4,4,128]{6,1,0,5,3,4,2:T(2,128)(2,1)S(1)}, u32[]{:S(2)}, u32[]{:S(2)}) collective-permute-start(bf16[3,2,1,2,4,4,128]{6,1,0,5,3,4,2:T(2,128)(2,1)S(1)} %get-tuple-element.34), channel_id=1, source_target_pairs={{0,12},{4,8},{8,4},{12,0},{1,13},{5,9},{9,5},{13,1},{2,14},{6,10},... | collective-permute-start | bytes 147464 | tf_op jit(solution)/shard_map/ppermute | solution.py:13
  23.1 0.8 %collective-permute-start.4 = (bf16[3,2,1,2,4,4,128]{6,1,0,5,3,4,2:T(2,128)(2,1)S(1)}, bf16[3,2,1,2,4,4,128]{6,1,0,5,3,4,2:T(2,128)(2,1)S(1)}, u32[]{:S(2)}, u32[]{:S(2)}) collective-permute-start(bf16[3,2,1,2,4,4,128]{6,1,0,5,3,4,2:T(2,128)(2,1)S(1)} %get-tuple-element.35), channel_id=1, source_target_pairs={{0,8},{4,12},{8,0},{12,4},{1,9},{5,13},{9,1},{13,5},{2,10},{6,14},... | collective-permute-start | bytes 147464 | tf_op jit(solution)/shard_map/ppermute | solution.py:13
  23.9 1.0 %fusion.20 = bf16[3,3,128,64]{2,3,1,0:T(8,128)(2,1)S(1)} fusion(f32[3,3,128,64]{2,3,1,0:T(8,128)S(1)} %fusion.62, f32[3,3,128,64]{2,3,1,0:T(8,128)S(1)} %convolution_add_fusion.1, bf16[1,3,3,128,512]{4,3,2,1,0:T(8,128)(2,1)S(1)} %get-tuple-element.5, s32[]{:T(128)S(6)} %select_n.138, bf16[64,128]{1,0:T(8,128)(2,1)} %collective-permute-done.13), kind=kOutput, calls=%fused_computation.23 | convolution fusion | flops 19095552 | bytes 1048580 | tf_op jit(solution)/shard_map/abdc,ec->abde/dot_general | solution.py:141
  25.7 1.1 %collective-permute-start.17 = (bf16[3,3,128,64]{2,3,1,0:T(8,128)(2,1)S(1)}, bf16[3,3,128,64]{2,3,1,0:T(8,128)(2,1)S(1)}, u32[]{:S(2)}, u32[]{:S(2)}) collective-permute-start(bf16[3,3,128,64]{2,3,1,0:T(8,128)(2,1)S(1)} %fusion.20), channel_id=1, source_target_pairs={{0,3},{1,2},{2,1},{3,0},{4,7},{5,6},{6,5},{7,4},{8,11},{9,10},{10,... | collective-permute-start | bytes 442376 | tf_op jit(solution)/shard_map/ppermute | solution.py:13
  26.8 0.8 %collective-permute-done.3 = bf16[3,2,1,2,4,4,128]{6,1,0,5,3,4,2:T(2,128)(2,1)S(1)} collective-permute-done((bf16[3,2,1,2,4,4,128]{6,1,0,5,3,4,2:T(2,128)(2,1)S(1)}, bf16[3,2,1,2,4,4,128]{6,1,0,5,3,4,2:T(2,128)(2,1)S(1)}, u32[]{:S(2)}, u32[]{:S(2)}) %collective-permute-start.3) | collective-permute-done | bytes 49184 | tf_op jit(solution)/shard_map/ppermute | solution.py:13
  27.6 1.1 %collective-permute-done.4 = bf16[3,2,1,2,4,4,128]{6,1,0,5,3,4,2:T(2,128)(2,1)S(1)} collective-permute-done((bf16[3,2,1,2,4,4,128]{6,1,0,5,3,4,2:T(2,128)(2,1)S(1)}, bf16[3,2,1,2,4,4,128]{6,1,0,5,3,4,2:T(2,128)(2,1)S(1)}, u32[]{:S(2)}, u32[]{:S(2)}) %collective-permute-start.4) | collective-permute-done | bytes 49184 | tf_op jit(solution)/shard_map/ppermute | solution.py:13
  30.4 1.6 %collective-permute-start.6 = (bf16[1,6,16,256]{3,2,1,0:T(8,128)(2,1)S(1)}, bf16[1,6,16,256]{3,2,1,0:T(8,128)(2,1)S(1)}, u32[]{:S(2)}, u32[]{:S(2)}) collective-permute-start(bf16[1,6,16,256]{3,2,1,0:T(8,128)(2,1)S(1)} %get-tuple-element.42), channel_id=1, source_target_pairs={{0,4},{4,0},{8,12},{12,8},{1,5},{5,1},{9,13},{13,9},{2,6},{6,2},{1... | collective-permute-start | bytes 147464 | tf_op jit(solution)/shard_map/ppermute | solution.py:13
  31.9 1.3 %collective-permute-start.8 = (bf16[1,6,16,256]{3,2,1,0:T(8,128)(2,1)S(1)}, bf16[1,6,16,256]{3,2,1,0:T(8,128)(2,1)S(1)}, u32[]{:S(2)}, u32[]{:S(2)}) collective-permute-start(bf16[1,6,16,256]{3,2,1,0:T(8,128)(2,1)S(1)} %get-tuple-element.43), channel_id=1, source_target_pairs={{0,12},{4,8},{8,4},{12,0},{1,13},{5,9},{9,5},{13,1},{2,14},{6,10},... | collective-permute-start | bytes 147464 | tf_op jit(solution)/shard_map/ppermute | solution.py:13
  33.3 1.2 %collective-permute-done.6 = bf16[1,6,16,256]{3,2,1,0:T(8,128)(2,1)S(1)} collective-permute-done((bf16[1,6,16,256]{3,2,1,0:T(8,128)(2,1)S(1)}, bf16[1,6,16,256]{3,2,1,0:T(8,128)(2,1)S(1)}, u32[]{:S(2)}, u32[]{:S(2)}) %collective-permute-start.6) | collective-permute-done | bytes 49184 | tf_op jit(solution)/shard_map/ppermute | solution.py:13
  34.5 1.7 %collective-permute-start.7 = (bf16[1,6,16,256]{3,2,1,0:T(8,128)(2,1)S(1)}, bf16[1,6,16,256]{3,2,1,0:T(8,128)(2,1)S(1)}, u32[]{:S(2)}, u32[]{:S(2)}) collective-permute-start(bf16[1,6,16,256]{3,2,1,0:T(8,128)(2,1)S(1)} %get-tuple-element.41), channel_id=1, source_target_pairs={{0,8},{4,12},{8,0},{12,4},{1,9},{5,13},{9,1},{13,5},{2,10},{6,14},... | collective-permute-start | bytes 147464 | tf_op jit(solution)/shard_map/ppermute | solution.py:13
  36.4 1.4 %collective-permute-done.8 = bf16[1,6,16,256]{3,2,1,0:T(8,128)(2,1)S(1)} collective-permute-done((bf16[1,6,16,256]{3,2,1,0:T(8,128)(2,1)S(1)}, bf16[1,6,16,256]{3,2,1,0:T(8,128)(2,1)S(1)}, u32[]{:S(2)}, u32[]{:S(2)}) %collective-permute-start.8) | collective-permute-done | bytes 49184 | tf_op jit(solution)/shard_map/ppermute | solution.py:13
  38.0 1.6 %collective-permute-done.7 = bf16[1,6,16,256]{3,2,1,0:T(8,128)(2,1)S(1)} collective-permute-done((bf16[1,6,16,256]{3,2,1,0:T(8,128)(2,1)S(1)}, bf16[1,6,16,256]{3,2,1,0:T(8,128)(2,1)S(1)}, u32[]{:S(2)}, u32[]{:S(2)}) %collective-permute-start.7) | collective-permute-done | bytes 49184 | tf_op jit(solution)/shard_map/ppermute | solution.py:13
  40.3 1.6 %collective-permute-start.9 = (bf16[1,6,16,256]{3,2,1,0:T(8,128)(2,1)S(1)}, bf16[1,6,16,256]{3,2,1,0:T(8,128)(2,1)S(1)}, u32[]{:S(2)}, u32[]{:S(2)}) collective-permute-start(bf16[1,6,16,256]{3,2,1,0:T(8,128)(2,1)S(1)} %fusion.29), channel_id=1, source_target_pairs={{0,1},{1,0},{2,3},{3,2},{4,5},{5,4},{6,7},{7,6},{8,9},{9,8},{10,11... | collective-permute-start | bytes 147464 | tf_op jit(solution)/shard_map/ppermute | solution.py:13
  42.1 2.3 %collective-permute-done.10 = bf16[1,6,16,256]{3,2,1,0:T(8,128)(2,1)S(1)} collective-permute-done((bf16[1,6,16,256]{3,2,1,0:T(8,128)(2,1)S(1)}, bf16[1,6,16,256]{3,2,1,0:T(8,128)(2,1)S(1)}, u32[]{:S(2)}, u32[]{:S(2)}) %collective-permute-start.10) | collective-permute-done | bytes 49184 | tf_op jit(solution)/shard_map/ppermute | solution.py:13
  45.6 2.2 %select_convert_fusion.1 = bf16[8,8,5,128]{3,1,2,0:T(8,128)(2,1)S(1)} fusion(bf16[4,3,3,128,512]{4,3,2,1,0:T(8,128)(2,1)} %param.7, bf16[10,1,7,1,512]{4,2,3,0,1:T(8,128)(2,1)S(1)} %get-tuple-element.21, bf16[10,1,7,1,512]{4,2,3,0,1:T(8,128)(2,1)S(1)} %get-tuple-element.20, bf16[10,1,8,5,512]{4,2,3,0,1:T(8,128)(2,1)S(1)} %fusion.35, ...), kind=kOutput, calls=%fused_computation.100 | convolution fusion | flops 380600320 | bytes 1814536 | tf_op jit(solution)/shard_map/conv_general_dilated | solution.py:114
  48.4 0.8 %collective-permute-start.19 = (bf16[1,8,32,128]{3,1,2,0:T(8,128)(2,1)S(1)}, bf16[1,8,32,128]{3,1,2,0:T(8,128)(2,1)S(1)}, u32[]{:S(2)}, u32[]{:S(2)}) collective-permute-start(bf16[1,8,32,128]{3,1,2,0:T(8,128)(2,1)S(1)} %slice_bitcast_fusion.1), channel_id=1, source_target_pairs={{0,2},{1,3},{2,0},{3,1},{4,6},{5,7},{6,4},{7,5},{8,10},{9,11},{10,... | collective-permute-start | bytes 196616 | tf_op jit(solution)/shard_map/ppermute | solution.py:13
  49.2 0.7 %collective-permute-start.20 = (bf16[1,8,32,128]{3,1,2,0:T(8,128)(2,1)S(1)}, bf16[1,8,32,128]{3,1,2,0:T(8,128)(2,1)S(1)}, u32[]{:S(2)}, u32[]{:S(2)}) collective-permute-start(bf16[1,8,32,128]{3,1,2,0:T(8,128)(2,1)S(1)} %slice_bitcast_fusion.1), channel_id=1, source_target_pairs={{0,3},{1,2},{2,1},{3,0},{4,7},{5,6},{6,5},{7,4},{8,11},{9,10},{10,... | collective-permute-start | bytes 196616 | tf_op jit(solution)/shard_map/ppermute | solution.py:13
  49.9 3.2 %collective-permute-done.19 = bf16[1,8,32,128]{3,1,2,0:T(8,128)(2,1)S(1)} collective-permute-done((bf16[1,8,32,128]{3,1,2,0:T(8,128)(2,1)S(1)}, bf16[1,8,32,128]{3,1,2,0:T(8,128)(2,1)S(1)}, u32[]{:S(2)}, u32[]{:S(2)}) %collective-permute-start.19) | collective-permute-done | bytes 65568 | tf_op jit(solution)/shard_map/ppermute | solution.py:13
  53.8 0.8 %select_convert_fusion.2 = bf16[6,8,5,128]{3,1,2,0:T(8,128)(2,1)S(1)} fusion(bf16[3,3,128,128]{3,2,1,0:T(8,128)(2,1)S(1)} %copy-done.7, bf16[3,3,128,128]{3,2,1,0:T(8,128)(2,1)S(1)} %copy-done.6, bf16[3,3,128,128]{3,2,1,0:T(8,128)(2,1)S(1)} %copy-done.5, bf16[3,3,128,128]{3,2,1,0:T(8,128)(2,1)S(1)} %copy-done.8, ...), kind=kOutput, calls=%fused_computation.112 | convolution fusion | flops 289425408 | bytes 1683502 | tf_op jit(solution)/shard_map/conv_general_dilated | solution.py:114
  55.0 1.0 %collective-permute-start.22 = (bf16[1,6,32,128]{3,1,2,0:T(8,128)(2,1)S(1)}, bf16[1,6,32,128]{3,1,2,0:T(8,128)(2,1)S(1)}, u32[]{:S(2)}, u32[]{:S(2)}) collective-permute-start(bf16[1,6,32,128]{3,1,2,0:T(8,128)(2,1)S(1)} %slice_bitcast_fusion), channel_id=1, source_target_pairs={{0,2},{1,3},{2,0},{3,1},{4,6},{5,7},{6,4},{7,5},{8,10},{9,11},{10,... | collective-permute-start | bytes 147464 | tf_op jit(solution)/shard_map/ppermute | solution.py:13
  56.6 2.9 %collective-permute-done.22 = bf16[1,6,32,128]{3,1,2,0:T(8,128)(2,1)S(1)} collective-permute-done((bf16[1,6,32,128]{3,1,2,0:T(8,128)(2,1)S(1)}, bf16[1,6,32,128]{3,1,2,0:T(8,128)(2,1)S(1)}, u32[]{:S(2)}, u32[]{:S(2)}) %collective-permute-start.22) | collective-permute-done | bytes 49184 | tf_op jit(solution)/shard_map/ppermute | solution.py:13
  59.5 0.9 %collective-permute-done.23 = bf16[1,6,32,128]{3,1,2,0:T(8,128)(2,1)S(1)} collective-permute-done((bf16[1,6,32,128]{3,1,2,0:T(8,128)(2,1)S(1)}, bf16[1,6,32,128]{3,1,2,0:T(8,128)(2,1)S(1)}, u32[]{:S(2)}, u32[]{:S(2)}) %collective-permute-start.23) | collective-permute-done | bytes 49184 | tf_op jit(solution)/shard_map/ppermute | solution.py:13
  (102 shorter events, 10.1 us)
Async XLA Ops:
  0.0 33.2 %copy-start = (bf16[4096,256]{1,0:T(8,128)(2,1)S(1)}, bf16[4096,256]{1,0:T(8,128)(2,1)}, u32[]{:S(2)}) copy-start(bf16[4096,256]{1,0:T(8,128)(2,1)} %param.5) | copy-start | bytes 6291460
  0.0 14.6 %collective-permute-start.12 = (bf16[64,128]{1,0:T(8,128)(2,1)}, bf16[64,128]{1,0:T(8,128)(2,1)S(1)}, u32[]{:S(2)}, u32[]{:S(2)}) collective-permute-start(bf16[64,128]{1,0:T(8,128)(2,1)} %param.6), channel_id=1, source_target_pairs={{0,1},{1,0},{2,3},{3,2},{4,5},{5,4},{6,7},{7,6},{8,9},{9,8},{10,11... | collective-permute-start | bytes 49160 | tf_op jit(solution)/shard_map/ppermute | solution.py:13
  0.5 15.5 %collective-permute-start.14 = (bf16[64,128]{1,0:T(8,128)(2,1)}, bf16[64,128]{1,0:T(8,128)(2,1)}, u32[]{:S(2)}, u32[]{:S(2)}) collective-permute-start(bf16[64,128]{1,0:T(8,128)(2,1)} %param.6), channel_id=1, source_target_pairs={{0,3},{1,2},{2,1},{3,0},{4,7},{5,6},{6,5},{7,4},{8,11},{9,10},{10,... | collective-permute-start | bytes 49160 | tf_op jit(solution)/shard_map/ppermute | solution.py:13
  3.1 20.8 %collective-permute-start.13 = (bf16[64,128]{1,0:T(8,128)(2,1)}, bf16[64,128]{1,0:T(8,128)(2,1)}, u32[]{:S(2)}, u32[]{:S(2)}) collective-permute-start(bf16[64,128]{1,0:T(8,128)(2,1)} %param.6), channel_id=1, source_target_pairs={{0,2},{1,3},{2,0},{3,1},{4,6},{5,7},{6,4},{7,5},{8,10},{9,11},{10,... | collective-permute-start | bytes 49160 | tf_op jit(solution)/shard_map/ppermute | solution.py:13
  4.0 12.9 %collective-permute-start = (bf16[1,2,4,3,8,128]{5,4,3,2,1,0:T(8,128)(2,1)S(1)}, bf16[1,2,4,3,8,128]{5,4,3,2,1,0:T(8,128)(2,1)S(1)}, u32[]{:S(2)}, u32[]{:S(2)}) collective-permute-start(bf16[1,2,4,3,8,128]{5,4,3,2,1,0:T(8,128)(2,1)S(1)} %get-tuple-element.38), channel_id=1, source_target_pairs={{0,1},{1,0},{2,3},{3,2},{4,5},{5,4},{6,7},{7,6},{8,9},{9,8},{10,11... | collective-permute-start | bytes 147464 | tf_op jit(solution)/shard_map/ppermute | solution.py:13
  4.2 12.7 %collective-permute-start.1 = (bf16[1,2,4,3,8,128]{5,4,3,2,1,0:T(8,128)(2,1)S(1)}, bf16[1,2,4,3,8,128]{5,4,3,2,1,0:T(8,128)(2,1)}, u32[]{:S(2)}, u32[]{:S(2)}) collective-permute-start(bf16[1,2,4,3,8,128]{5,4,3,2,1,0:T(8,128)(2,1)S(1)} %get-tuple-element.40), channel_id=1, source_target_pairs={{0,2},{1,3},{2,0},{3,1},{4,6},{5,7},{6,4},{7,5},{8,10},{9,11},{10,... | collective-permute-start | bytes 147464 | tf_op jit(solution)/shard_map/ppermute | solution.py:13
  14.6 3.8 %collective-permute-start.2 = (bf16[1,2,4,3,8,128]{5,4,3,2,1,0:T(8,128)(2,1)S(1)}, bf16[1,2,4,3,8,128]{5,4,3,2,1,0:T(8,128)(2,1)S(1)}, u32[]{:S(2)}, u32[]{:S(2)}) collective-permute-start(bf16[1,2,4,3,8,128]{5,4,3,2,1,0:T(8,128)(2,1)S(1)} %get-tuple-element.39), channel_id=1, source_target_pairs={{0,3},{1,2},{2,1},{3,0},{4,7},{5,6},{6,5},{7,4},{8,11},{9,10},{10,... | collective-permute-start | bytes 147464 | tf_op jit(solution)/shard_map/ppermute | solution.py:13
  19.5 6.3 %collective-permute-start.5 = (bf16[3,2,1,2,4,4,128]{6,1,0,5,3,4,2:T(2,128)(2,1)S(1)}, bf16[3,2,1,2,4,4,128]{6,1,0,5,3,4,2:T(2,128)(2,1)S(1)}, u32[]{:S(2)}, u32[]{:S(2)}) collective-permute-start(bf16[3,2,1,2,4,4,128]{6,1,0,5,3,4,2:T(2,128)(2,1)S(1)} %get-tuple-element.34), channel_id=1, source_target_pairs={{0,12},{4,8},{8,4},{12,0},{1,13},{5,9},{9,5},{13,1},{2,14},{6,10},... | collective-permute-start | bytes 147464 | tf_op jit(solution)/shard_map/ppermute | solution.py:13
  23.1 4.4 %collective-permute-start.3 = (bf16[3,2,1,2,4,4,128]{6,1,0,5,3,4,2:T(2,128)(2,1)S(1)}, bf16[3,2,1,2,4,4,128]{6,1,0,5,3,4,2:T(2,128)(2,1)S(1)}, u32[]{:S(2)}, u32[]{:S(2)}) collective-permute-start(bf16[3,2,1,2,4,4,128]{6,1,0,5,3,4,2:T(2,128)(2,1)S(1)} %get-tuple-element.36), channel_id=1, source_target_pairs={{0,4},{4,0},{8,12},{12,8},{1,5},{5,1},{9,13},{13,9},{2,6},{6,2},{1... | collective-permute-start | bytes 147464 | tf_op jit(solution)/shard_map/ppermute | solution.py:13
  23.1 5.5 %collective-permute-start.4 = (bf16[3,2,1,2,4,4,128]{6,1,0,5,3,4,2:T(2,128)(2,1)S(1)}, bf16[3,2,1,2,4,4,128]{6,1,0,5,3,4,2:T(2,128)(2,1)S(1)}, u32[]{:S(2)}, u32[]{:S(2)}) collective-permute-start(bf16[3,2,1,2,4,4,128]{6,1,0,5,3,4,2:T(2,128)(2,1)S(1)} %get-tuple-element.35), channel_id=1, source_target_pairs={{0,8},{4,12},{8,0},{12,4},{1,9},{5,13},{9,1},{13,5},{2,10},{6,14},... | collective-permute-start | bytes 147464 | tf_op jit(solution)/shard_map/ppermute | solution.py:13
  24.9 15.4 %collective-permute-start.15 = (bf16[3,3,128,64]{2,3,1,0:T(8,128)(2,1)S(1)}, bf16[3,3,128,64]{2,3,1,0:T(8,128)(2,1)S(1)}, u32[]{:S(2)}, u32[]{:S(2)}) collective-permute-start(bf16[3,3,128,64]{2,3,1,0:T(8,128)(2,1)S(1)} %fusion.20), channel_id=1, source_target_pairs={{0,1},{1,0},{2,3},{3,2},{4,5},{5,4},{6,7},{7,6},{8,9},{9,8},{10,11... | collective-permute-start | bytes 442376 | tf_op jit(solution)/shard_map/ppermute | solution.py:13
  24.9 16.9 %collective-permute-start.16 = (bf16[3,3,128,64]{2,3,1,0:T(8,128)(2,1)S(1)}, bf16[3,3,128,64]{2,3,1,0:T(8,128)(2,1)S(1)}, u32[]{:S(2)}, u32[]{:S(2)}) collective-permute-start(bf16[3,3,128,64]{2,3,1,0:T(8,128)(2,1)S(1)} %fusion.20), channel_id=1, source_target_pairs={{0,2},{1,3},{2,0},{3,1},{4,6},{5,7},{6,4},{7,5},{8,10},{9,11},{10,... | collective-permute-start | bytes 442376 | tf_op jit(solution)/shard_map/ppermute | solution.py:13
  25.7 16.2 %collective-permute-start.17 = (bf16[3,3,128,64]{2,3,1,0:T(8,128)(2,1)S(1)}, bf16[3,3,128,64]{2,3,1,0:T(8,128)(2,1)S(1)}, u32[]{:S(2)}, u32[]{:S(2)}) collective-permute-start(bf16[3,3,128,64]{2,3,1,0:T(8,128)(2,1)S(1)} %fusion.20), channel_id=1, source_target_pairs={{0,3},{1,2},{2,1},{3,0},{4,7},{5,6},{6,5},{7,4},{8,11},{9,10},{10,... | collective-permute-start | bytes 442376 | tf_op jit(solution)/shard_map/ppermute | solution.py:13
  30.4 4.2 %collective-permute-start.6 = (bf16[1,6,16,256]{3,2,1,0:T(8,128)(2,1)S(1)}, bf16[1,6,16,256]{3,2,1,0:T(8,128)(2,1)S(1)}, u32[]{:S(2)}, u32[]{:S(2)}) collective-permute-start(bf16[1,6,16,256]{3,2,1,0:T(8,128)(2,1)S(1)} %get-tuple-element.42), channel_id=1, source_target_pairs={{0,4},{4,0},{8,12},{12,8},{1,5},{5,1},{9,13},{13,9},{2,6},{6,2},{1... | collective-permute-start | bytes 147464 | tf_op jit(solution)/shard_map/ppermute | solution.py:13
  31.9 5.9 %collective-permute-start.8 = (bf16[1,6,16,256]{3,2,1,0:T(8,128)(2,1)S(1)}, bf16[1,6,16,256]{3,2,1,0:T(8,128)(2,1)S(1)}, u32[]{:S(2)}, u32[]{:S(2)}) collective-permute-start(bf16[1,6,16,256]{3,2,1,0:T(8,128)(2,1)S(1)} %get-tuple-element.43), channel_id=1, source_target_pairs={{0,12},{4,8},{8,4},{12,0},{1,13},{5,9},{9,5},{13,1},{2,14},{6,10},... | collective-permute-start | bytes 147464 | tf_op jit(solution)/shard_map/ppermute | solution.py:13
  34.5 5.0 %collective-permute-start.7 = (bf16[1,6,16,256]{3,2,1,0:T(8,128)(2,1)S(1)}, bf16[1,6,16,256]{3,2,1,0:T(8,128)(2,1)S(1)}, u32[]{:S(2)}, u32[]{:S(2)}) collective-permute-start(bf16[1,6,16,256]{3,2,1,0:T(8,128)(2,1)S(1)} %get-tuple-element.41), channel_id=1, source_target_pairs={{0,8},{4,12},{8,0},{12,4},{1,9},{5,13},{9,1},{13,5},{2,10},{6,14},... | collective-permute-start | bytes 147464 | tf_op jit(solution)/shard_map/ppermute | solution.py:13
  39.7 4.6 %collective-permute-start.10 = (bf16[1,6,16,256]{3,2,1,0:T(8,128)(2,1)S(1)}, bf16[1,6,16,256]{3,2,1,0:T(8,128)(2,1)S(1)}, u32[]{:S(2)}, u32[]{:S(2)}) collective-permute-start(bf16[1,6,16,256]{3,2,1,0:T(8,128)(2,1)S(1)} %fusion.29), channel_id=1, source_target_pairs={{0,2},{1,3},{2,0},{3,1},{4,6},{5,7},{6,4},{7,5},{8,10},{9,11},{10,... | collective-permute-start | bytes 147464 | tf_op jit(solution)/shard_map/ppermute | solution.py:13
  40.3 4.0 %collective-permute-start.11 = (bf16[1,6,16,256]{3,2,1,0:T(8,128)(2,1)S(1)}, bf16[1,6,16,256]{3,2,1,0:T(8,128)(2,1)S(1)}, u32[]{:S(2)}, u32[]{:S(2)}) collective-permute-start(bf16[1,6,16,256]{3,2,1,0:T(8,128)(2,1)S(1)} %fusion.29), channel_id=1, source_target_pairs={{0,3},{1,2},{2,1},{3,0},{4,7},{5,6},{6,5},{7,4},{8,11},{9,10},{10,... | collective-permute-start | bytes 147464 | tf_op jit(solution)/shard_map/ppermute | solution.py:13
  40.3 4.0 %collective-permute-start.9 = (bf16[1,6,16,256]{3,2,1,0:T(8,128)(2,1)S(1)}, bf16[1,6,16,256]{3,2,1,0:T(8,128)(2,1)S(1)}, u32[]{:S(2)}, u32[]{:S(2)}) collective-permute-start(bf16[1,6,16,256]{3,2,1,0:T(8,128)(2,1)S(1)} %fusion.29), channel_id=1, source_target_pairs={{0,1},{1,0},{2,3},{3,2},{4,5},{5,4},{6,7},{7,6},{8,9},{9,8},{10,11... | collective-permute-start | bytes 147464 | tf_op jit(solution)/shard_map/ppermute | solution.py:13
  47.9 5.9 %copy-start.5 = (bf16[3,3,128,128]{3,2,1,0:T(8,128)(2,1)S(1)}, bf16[3,3,128,128]{3,2,1,0:T(8,128)(2,1)}, u32[]{:S(2)}) copy-start(bf16[3,3,128,128]{3,2,1,0:T(8,128)(2,1)} %get-tuple-element.50) | copy-start | bytes 884740
  47.9 5.9 %copy-start.6 = (bf16[3,3,128,128]{3,2,1,0:T(8,128)(2,1)S(1)}, bf16[3,3,128,128]{3,2,1,0:T(8,128)(2,1)}, u32[]{:S(2)}) copy-start(bf16[3,3,128,128]{3,2,1,0:T(8,128)(2,1)} %get-tuple-element.51) | copy-start | bytes 884740
  47.9 5.9 %copy-start.7 = (bf16[3,3,128,128]{3,2,1,0:T(8,128)(2,1)S(1)}, bf16[3,3,128,128]{3,2,1,0:T(8,128)(2,1)}, u32[]{:S(2)}) copy-start(bf16[3,3,128,128]{3,2,1,0:T(8,128)(2,1)} %get-tuple-element.52) | copy-start | bytes 884740
  48.0 1.9 %collective-permute-start.18 = (bf16[1,8,32,128]{3,1,2,0:T(8,128)(2,1)S(1)}, bf16[1,8,32,128]{3,1,2,0:T(8,128)(2,1)S(1)}, u32[]{:S(2)}, u32[]{:S(2)}) collective-permute-start(bf16[1,8,32,128]{3,1,2,0:T(8,128)(2,1)S(1)} %slice_bitcast_fusion.1), channel_id=1, source_target_pairs={{0,1},{1,0},{2,3},{3,2},{4,5},{5,4},{6,7},{7,6},{8,9},{9,8},{10,11... | collective-permute-start | bytes 196616 | tf_op jit(solution)/shard_map/ppermute | solution.py:13
  48.4 4.7 %collective-permute-start.19 = (bf16[1,8,32,128]{3,1,2,0:T(8,128)(2,1)S(1)}, bf16[1,8,32,128]{3,1,2,0:T(8,128)(2,1)S(1)}, u32[]{:S(2)}, u32[]{:S(2)}) collective-permute-start(bf16[1,8,32,128]{3,1,2,0:T(8,128)(2,1)S(1)} %slice_bitcast_fusion.1), channel_id=1, source_target_pairs={{0,2},{1,3},{2,0},{3,1},{4,6},{5,7},{6,4},{7,5},{8,10},{9,11},{10,... | collective-permute-start | bytes 196616 | tf_op jit(solution)/shard_map/ppermute | solution.py:13
  49.2 4.4 %collective-permute-start.20 = (bf16[1,8,32,128]{3,1,2,0:T(8,128)(2,1)S(1)}, bf16[1,8,32,128]{3,1,2,0:T(8,128)(2,1)S(1)}, u32[]{:S(2)}, u32[]{:S(2)}) collective-permute-start(bf16[1,8,32,128]{3,1,2,0:T(8,128)(2,1)S(1)} %slice_bitcast_fusion.1), channel_id=1, source_target_pairs={{0,3},{1,2},{2,1},{3,0},{4,7},{5,6},{6,5},{7,4},{8,11},{9,10},{10,... | collective-permute-start | bytes 196616 | tf_op jit(solution)/shard_map/ppermute | solution.py:13
  54.6 6.1 %copy-start.1 = (bf16[3,3,128,128]{3,2,1,0:T(8,128)(2,1)S(1)}, bf16[3,3,128,128]{3,2,1,0:T(8,128)(2,1)}, u32[]{:S(2)}) copy-start(bf16[3,3,128,128]{3,2,1,0:T(8,128)(2,1)} %get-tuple-element.12) | copy-start | bytes 884740
  54.6 6.1 %copy-start.2 = (bf16[3,3,128,128]{3,2,1,0:T(8,128)(2,1)S(1)}, bf16[3,3,128,128]{3,2,1,0:T(8,128)(2,1)}, u32[]{:S(2)}) copy-start(bf16[3,3,128,128]{3,2,1,0:T(8,128)(2,1)} %get-tuple-element.13) | copy-start | bytes 884740
  54.6 6.1 %copy-start.3 = (bf16[3,3,128,128]{3,2,1,0:T(8,128)(2,1)S(1)}, bf16[3,3,128,128]{3,2,1,0:T(8,128)(2,1)}, u32[]{:S(2)}) copy-start(bf16[3,3,128,128]{3,2,1,0:T(8,128)(2,1)} %get-tuple-element.14) | copy-start | bytes 884740
  54.6 6.1 %copy-start.4 = (bf16[3,3,128,128]{3,2,1,0:T(8,128)(2,1)S(1)}, bf16[3,3,128,128]{3,2,1,0:T(8,128)(2,1)}, u32[]{:S(2)}) copy-start(bf16[3,3,128,128]{3,2,1,0:T(8,128)(2,1)} %get-tuple-element.15) | copy-start | bytes 884740
  54.7 1.9 %collective-permute-start.21 = (bf16[1,6,32,128]{3,1,2,0:T(8,128)(2,1)S(1)}, bf16[1,6,32,128]{3,1,2,0:T(8,128)(2,1)S(1)}, u32[]{:S(2)}, u32[]{:S(2)}) collective-permute-start(bf16[1,6,32,128]{3,1,2,0:T(8,128)(2,1)S(1)} %slice_bitcast_fusion), channel_id=1, source_target_pairs={{0,1},{1,0},{2,3},{3,2},{4,5},{5,4},{6,7},{7,6},{8,9},{9,8},{10,11... | collective-permute-start | bytes 147464 | tf_op jit(solution)/shard_map/ppermute | solution.py:13
  55.0 4.5 %collective-permute-start.22 = (bf16[1,6,32,128]{3,1,2,0:T(8,128)(2,1)S(1)}, bf16[1,6,32,128]{3,1,2,0:T(8,128)(2,1)S(1)}, u32[]{:S(2)}, u32[]{:S(2)}) collective-permute-start(bf16[1,6,32,128]{3,1,2,0:T(8,128)(2,1)S(1)} %slice_bitcast_fusion), channel_id=1, source_target_pairs={{0,2},{1,3},{2,0},{3,1},{4,6},{5,7},{6,4},{7,5},{8,10},{9,11},{10,... | collective-permute-start | bytes 147464 | tf_op jit(solution)/shard_map/ppermute | solution.py:13
  56.1 4.4 %collective-permute-start.23 = (bf16[1,6,32,128]{3,1,2,0:T(8,128)(2,1)S(1)}, bf16[1,6,32,128]{3,1,2,0:T(8,128)(2,1)S(1)}, u32[]{:S(2)}, u32[]{:S(2)}) collective-permute-start(bf16[1,6,32,128]{3,1,2,0:T(8,128)(2,1)S(1)} %slice_bitcast_fusion), channel_id=1, source_target_pairs={{0,3},{1,2},{2,1},{3,0},{4,7},{5,6},{6,5},{7,4},{8,11},{9,10},{10,... | collective-permute-start | bytes 147464 | tf_op jit(solution)/shard_map/ppermute | solution.py:13
  (4 other events, 16.0 us)
